TPU v7x, 32 devices: a whole 2x2x4 slice. The times are simulated.
32 devices in a mesh: src: 16 (over z, y, core), tgt: 2 (over x).
Axes of the slice: x: 2, y: 2, z: 4, core: 2. Of those that a mesh axis runs over, the one named last changes fastest.
Arguments:
- positions: float32 [3, 4096], P(None, ('src', 'tgt')), may hold values from -1.3 to 1.3, as said below
- areas: float32 [4096], P(('src', 'tgt')), may hold values from 0.25 to 4
- right_side: float32 [3, 4096], P(None, ('src', 'tgt')), may hold values from -6 to 6
Outputs:
- solution_field: float32 [3, 4096], P(None, ('src', 'tgt'))
- residual: float32 [3, 4096], P(None, ('src', 'tgt'))
- hessenberg: float32 [5, 4], replicated
Inputs may be any that keep to these rules, and one draw needn't show every extreme that they name: positions lie on a sphere of radius 1 or an ellipsoid centred at the anchor with semi-axes between 0.7 and 1.3, with no locality in how panels are assigned to devices.
All inputs are finite; a program needn't handle non-finite values.
Results may differ from a plain program's by a relative error of at most 0.0003.
Values sent between devices are 32-bit elements.
A program may use at most 64 MiB of HBM per device.

v0:
```python
import math

import jax
import jax.numpy as jnp
from jax import lax
from jax.sharding import PartitionSpec as P

ITERS = 4


soften = 0.0025
column_block = 2048


def stokes_block(targets, sources, densities):
    offset = targets[:, :, None] - sources[:, None, :]
    square = jnp.sum(offset * offset, axis=0) + soften
    factor = square ** (-1.5)
    projected = jnp.sum(offset * densities[:, None, :], axis=0)
    return jnp.sum(
        factor[None] * ((square + soften)[None] * densities[:, None, :] + offset * projected[None]),
        axis=2,
    )


def stokes_sum(targets, sources, densities):
    columns = sources.shape[1]
    stride = math.gcd(columns, column_block)
    blocks = columns // stride
    if blocks == 1:
        return stokes_block(targets, sources, densities)
    source_blocks = sources.reshape(3, blocks, stride).transpose(1, 0, 2)
    density_blocks = densities.reshape(3, blocks, stride).transpose(1, 0, 2)

    def accumulate(accumulated, block_pair):
        return (accumulated + stokes_block(targets, block_pair[0], block_pair[1]), None)

    accumulated, unused = lax.scan(
        accumulate, jnp.zeros((3, targets.shape[1]), jnp.float32), (source_blocks, density_blocks)
    )
    return accumulated


def least_squares(hessenberg, initial):
    columns = hessenberg.shape[1]
    triangle = hessenberg
    target = jnp.zeros((hessenberg.shape[0],), jnp.float32).at[0].set(initial)
    for column in range(columns):
        leading = triangle[column, column]
        second = triangle[column + 1, column]
        radius = jnp.sqrt(leading * leading + second * second)
        cosine = leading / radius
        sine_value = second / radius
        row_top = triangle[column]
        row_low = triangle[column + 1]
        triangle = triangle.at[column].set(cosine * row_top + sine_value * row_low)
        triangle = triangle.at[column + 1].set(cosine * row_low - sine_value * row_top)
        target_top = target[column]
        target_low = target[column + 1]
        target = target.at[column].set(cosine * target_top + sine_value * target_low)
        target = target.at[column + 1].set(cosine * target_low - sine_value * target_top)
    solution = jnp.zeros((columns,), jnp.float32)
    for row_index in reversed(range(columns)):
        partial_sum = jnp.sum(
            triangle[row_index, row_index + 1 : columns] * solution[row_index + 1 : columns]
        )
        solution = solution.at[row_index].set(
            (target[row_index] - partial_sum) / triangle[row_index, row_index]
        )
    return solution


def local(positions, areas, right_side):
    device_count = lax.axis_size("src") * lax.axis_size("tgt")
    coefficient = float(positions.shape[1] * device_count) ** (-0.5)
    weights = areas * coefficient
    every_position = lax.all_gather(positions, ("src", "tgt"), axis=1, tiled=True)

    def apply_operator(vector):
        weighted = vector * weights[None, :]
        pair_loads = lax.all_gather(weighted, "tgt", axis=1, tiled=True)

        def absorb(accumulated, piece):
            sources = lax.slice_in_dim(every_position, 0, piece.shape[1], axis=1)
            return accumulated + stokes_sum(positions, sources, piece)

        induced = absorb(
            jnp.zeros_like(vector),
            jax.tree.map(lambda a: lax.all_gather(a, "src", axis=1, tiled=True), pair_loads),
        )
        return vector + induced

    initial = jnp.sqrt(lax.psum(jnp.sum(right_side * right_side), ("src", "tgt")))
    krylov_basis = [right_side / initial]
    hessenberg = jnp.zeros((ITERS + 1, ITERS), jnp.float32)
    for iteration in range(ITERS):
        applied = apply_operator(krylov_basis[iteration])
        stacked = jnp.stack(krylov_basis)
        projections = lax.psum(jnp.sum(stacked * applied[None], axis=(1, 2)), ("src", "tgt"))
        remainder = applied - jnp.sum(projections[:, None, None] * stacked, axis=0)
        height = jnp.sqrt(lax.psum(jnp.sum(remainder * remainder), ("src", "tgt")))
        hessenberg = hessenberg.at[: iteration + 1, iteration].set(projections)
        hessenberg = hessenberg.at[iteration + 1, iteration].set(height)
        krylov_basis.append(remainder / height)
    coefficients = least_squares(hessenberg, initial)
    stacked = jnp.stack(krylov_basis)
    solution_field = jnp.sum(coefficients[:, None, None] * stacked[:ITERS], axis=0)
    misfit = -jnp.sum(hessenberg * coefficients[None, :], axis=1)
    misfit = misfit.at[0].add(initial)
    residual = jnp.sum(misfit[:, None, None] * stacked, axis=0)
    return (solution_field, residual, hessenberg)


def solution(mesh):
    return jax.shard_map(
        local,
        mesh=mesh,
        in_specs=(P(None, ("src", "tgt")), P(("src", "tgt")), P(None, ("src", "tgt"))),
        out_specs=(P(None, ("src", "tgt")), P(None, ("src", "tgt")), P()),
        check_vma=False,
    )
```

profile of v0, /device:TPU:0, one launch (start us, length us, event | category | flops | bytes accessed | tf_op | source)
XLA Modules:
  0.0 610.6 jit_solution(4597911787184220807)
XLA Ops:
  1.9 42.1 %psum.63 = f32[]{:T(128)} all-reduce(f32[]{:T(128)} %multiply_reduce_fusion.14), channel_id=1, replica_groups=mesh['src'=16,'tgt'=2] {'src','tgt'}, use_global_device_ids=true, to_apply=%region_1.0 | all-reduce | flops 1 | bytes 8 | tf_op jit(solution)/shard_map/psum | solution.py:93
  46.1 4.6 all_gather.28
  50.6 21.2 %all_gather.29 = f32[3,4096]{1,0:T(4,128)S(1)} all-gather(f32[3,256]{1,0:T(4,128)S(1)} %all_gather.28), channel_id=1, replica_groups=mesh['src'=16,'tgt'=2] {'src'}, dimensions={1}, use_global_device_ids=true | all-gather | bytes 52224 | tf_op jit(solution)/shard_map/all_gather | solution.py:89
  71.8 64.4 %all_gather.27 = f32[3,4096]{1,0:T(4,128)S(1)} all-gather(f32[3,128]{1,0:T(4,128)} %param.71), channel_id=1, replica_groups=mesh['src'=16,'tgt'=2] {'src','tgt'}, dimensions={1}, use_global_device_ids=true | all-gather | bytes 50688 | tf_op jit(solution)/shard_map/all_gather | solution.py:77
  136.2 6.7 %while.82 = (s32[]{:T(128)}, f32[3,128]{1,0:T(4,128)S(1)}, f32[3,128]{1,0:T(4,128)}, f32[2,3,2048]{2,1,0:T(4,128)S(1)}, f32[2,3,2048]{2,1,0:T(4,128)S(1)}, /*index=5*/s32[]{:T(128)}, s32[]{:T(128)}) while((s32[]{:T(128)}, f32[3,128]{1,0:T(4,128)S(1)}, f32[3,128]{1,0:T(4,128)}, f32[2,3,2048]{2,1,0:T(4,128)S(1)}, ...), condition=%wide.region_6.7_spmd.clone, body=%wide.region_2.6_spmd.clone.sunk | while | flops 8651139 | bytes 8600695 | solution.py:38
  136.2 1.8 fusion.41
  139.6 1.8 fusion.41
  143.5 37.1 %psum.64 = f32[1]{0:T(128)} all-reduce(f32[1]{0:T(128)} %bitcast.4), channel_id=1, replica_groups=mesh['src'=16,'tgt'=2] {'src','tgt'}, use_global_device_ids=true, to_apply=%region_8.9 | all-reduce | flops 1 | bytes 8 | tf_op jit(solution)/shard_map/psum | solution.py:99
  181.8 42.9 %psum.65 = f32[]{:T(128)} all-reduce(f32[]{:T(128)} %multiply_reduce_fusion.12), channel_id=1, replica_groups=mesh['src'=16,'tgt'=2] {'src','tgt'}, use_global_device_ids=true, to_apply=%region_10.11 | all-reduce | flops 1 | bytes 8 | tf_op jit(solution)/shard_map/psum | solution.py:101
  226.1 4.6 all_gather.30
  230.7 20.5 %all_gather.31 = f32[3,4096]{1,0:T(4,128)S(1)} all-gather(f32[3,256]{1,0:T(4,128)S(1)} %all_gather.30), channel_id=1, replica_groups=mesh['src'=16,'tgt'=2] {'src'}, dimensions={1}, use_global_device_ids=true | all-gather | bytes 52224 | tf_op jit(solution)/shard_map/all_gather | solution.py:89
  251.2 6.7 %while.83 = (s32[]{:T(128)}, f32[3,128]{1,0:T(4,128)S(1)}, f32[3,128]{1,0:T(4,128)}, f32[2,3,2048]{2,1,0:T(4,128)S(1)}, f32[2,3,2048]{2,1,0:T(4,128)S(1)}, /*index=5*/s32[]{:T(128)}, s32[]{:T(128)}) while((s32[]{:T(128)}, f32[3,128]{1,0:T(4,128)S(1)}, f32[3,128]{1,0:T(4,128)}, f32[2,3,2048]{2,1,0:T(4,128)S(1)}, ...), condition=%wide.region_16.0_spmd.clone, body=%wide.region_12.16_spmd.clone.sunk | while | flops 8651139 | bytes 8600695 | solution.py:38
  254.5 1.8 fusion.43
  258.0 36.8 %psum.66 = f32[2]{0:T(128)S(1)} all-reduce(f32[2]{0:T(128)S(1)} %multiply_reduce_fusion.7), channel_id=1, replica_groups=mesh['src'=16,'tgt'=2] {'src','tgt'}, use_global_device_ids=true, to_apply=%region_18.19 | all-reduce | flops 2 | bytes 16 | tf_op jit(solution)/shard_map/psum | solution.py:99
  295.5 41.3 %psum.67 = f32[]{:T(128)} all-reduce(f32[]{:T(128)} %get-tuple-element.753), channel_id=1, replica_groups=mesh['src'=16,'tgt'=2] {'src','tgt'}, use_global_device_ids=true, to_apply=%region_21.22 | all-reduce | flops 1 | bytes 8 | tf_op jit(solution)/shard_map/psum | solution.py:101
  337.5 4.6 all_gather.32
  342.1 20.5 %all_gather.33 = f32[3,4096]{1,0:T(4,128)S(1)} all-gather(f32[3,256]{1,0:T(4,128)S(1)} %all_gather.32), channel_id=1, replica_groups=mesh['src'=16,'tgt'=2] {'src'}, dimensions={1}, use_global_device_ids=true | all-gather | bytes 52224 | tf_op jit(solution)/shard_map/all_gather | solution.py:89
  362.5 6.7 %while.84 = (s32[]{:T(128)}, f32[3,128]{1,0:T(4,128)S(1)}, f32[3,128]{1,0:T(4,128)}, f32[2,3,2048]{2,1,0:T(4,128)S(1)}, f32[2,3,2048]{2,1,0:T(4,128)S(1)}, /*index=5*/s32[]{:T(128)}, s32[]{:T(128)}) while((s32[]{:T(128)}, f32[3,128]{1,0:T(4,128)S(1)}, f32[3,128]{1,0:T(4,128)}, f32[2,3,2048]{2,1,0:T(4,128)S(1)}, ...), condition=%wide.region_27.0_spmd.clone, body=%wide.region_23.27_spmd.clone.sunk | while | flops 8651139 | bytes 8600695 | solution.py:38
  362.5 1.8 fusion.45
  365.9 1.8 fusion.45
  369.4 37.1 %psum.68 = f32[3]{0:T(128)S(1)} all-reduce(f32[3]{0:T(128)S(1)} %multiply_reduce_fusion.5), channel_id=1, replica_groups=mesh['src'=16,'tgt'=2] {'src','tgt'}, use_global_device_ids=true, to_apply=%region_29.0 | all-reduce | flops 3 | bytes 24 | tf_op jit(solution)/shard_map/psum | solution.py:99
  407.2 42.6 %psum.69 = f32[]{:T(128)} all-reduce(f32[]{:T(128)} %get-tuple-element.751), channel_id=1, replica_groups=mesh['src'=16,'tgt'=2] {'src','tgt'}, use_global_device_ids=true, to_apply=%region_32.33 | all-reduce | flops 1 | bytes 8 | tf_op jit(solution)/shard_map/psum | solution.py:101
  450.5 4.6 all_gather.34
  455.1 20.5 %all_gather.35 = f32[3,4096]{1,0:T(4,128)S(1)} all-gather(f32[3,256]{1,0:T(4,128)S(1)} %all_gather.34), channel_id=1, replica_groups=mesh['src'=16,'tgt'=2] {'src'}, dimensions={1}, use_global_device_ids=true | all-gather | bytes 52224 | tf_op jit(solution)/shard_map/all_gather | solution.py:89
  475.6 6.7 %while.85 = (s32[]{:T(128)}, f32[3,128]{1,0:T(4,128)S(1)}, f32[3,128]{1,0:T(4,128)}, f32[2,3,2048]{2,1,0:T(4,128)S(1)}, f32[2,3,2048]{2,1,0:T(4,128)S(1)}, /*index=5*/s32[]{:T(128)}, s32[]{:T(128)}) while((s32[]{:T(128)}, f32[3,128]{1,0:T(4,128)S(1)}, f32[3,128]{1,0:T(4,128)}, f32[2,3,2048]{2,1,0:T(4,128)S(1)}, ...), condition=%wide.region_38.39_spmd.clone, body=%wide.region_34.38_spmd.clone.sunk | while | flops 8651139 | bytes 8600695 | solution.py:38
  475.7 1.8 fusion.47
  479.0 1.8 fusion.47
  482.5 36.8 %psum.70 = f32[4]{0:T(128)S(1)} all-reduce(f32[4]{0:T(128)S(1)} %multiply_reduce_fusion.3), channel_id=1, replica_groups=mesh['src'=16,'tgt'=2] {'src','tgt'}, use_global_device_ids=true, to_apply=%region_40.0 | all-reduce | flops 4 | bytes 32 | tf_op jit(solution)/shard_map/psum | solution.py:99
  520.1 41.3 %psum.71 = f32[]{:T(128)} all-reduce(f32[]{:T(128)} %get-tuple-element.749), channel_id=1, replica_groups=mesh['src'=16,'tgt'=2] {'src','tgt'}, use_global_device_ids=true, to_apply=%region_43.44 | all-reduce | flops 1 | bytes 8 | tf_op jit(solution)/shard_map/psum | solution.py:101
  564.1 2.1 broadcast_select_fusion.2
  569.0 2.1 broadcast_select_fusion.1
  573.9 2.1 broadcast_select_fusion
  (134 shorter events, 40.4 us)
Async XLA Ops:
  136.2 6.7 %copy-start.5 = (f32[3,128]{1,0:T(4,128)S(1)}, f32[3,128]{1,0:T(4,128)}, u32[]{:S(2)}) copy-start(f32[3,128]{1,0:T(4,128)} %param.73) | copy-start | bytes 4612
  138.0 0.7 copy-start
  141.4 0.7 copy-start
  253.0 0.7 copy-start.1
  256.4 0.7 copy-start.1
  364.4 0.7 copy-start.2
  367.7 0.7 copy-start.2
  475.6 92.7 %copy-start.7 = (s32[2]{0:T(128)S(1)}, s32[2]{0:T(128)}, u32[]{:S(2)}) copy-start(s32[2]{0:T(128)} %constant.812.clone.1) | copy-start | bytes 28
  475.6 97.6 %copy-start.6 = (s32[2]{0:T(128)S(1)}, s32[2]{0:T(128)}, u32[]{:S(2)}) copy-start(s32[2]{0:T(128)} %constant.813.clone.1) | copy-start | bytes 28
  477.5 0.7 copy-start.3
  480.9 0.7 copy-start.3
  577.6 33.0 %copy-start.4 = (f32[5,4]{0,1:T(4,128)}, f32[5,4]{0,1:T(4,128)S(1)}, u32[]{:S(2)}) copy-start(f32[5,4]{0,1:T(4,128)S(1)} %scatter.61) | copy-start | bytes 244
where the time goes:
time: 613 us; the launch traced here: 611 us
  blocking collectives  523 us (85%)
  other arithmetic  43.4 us (7%)
  between operations  27.7 us (5%)
  local copies, waits for them, and re-layouts  15.9 us (3%)
    psum x4, blocking collectives, local(): height = jnp.sqrt(lax.psum(jnp.sum(remainder * remainder), ('src', 'tgt')))  168 us
    psum x4, blocking collectives, local(): lax.psum(jnp.sum(stacked * applied[None], axis=(1, 2)), ('src', 'tgt'))  148 us
    all_gather x4, blocking collectives, apply_operator(): lax.all_gather(a, 'src', axis=1, tiled=True)  82.6 us
    all_gather x1, blocking collectives, local(): lax.all_gather(positions, ('src', 'tgt'), axis=1, tiled=True)  64.4 us
    psum x1, blocking collectives, local(): lax.psum(jnp.sum(right_side * right_side), ('src', 'tgt'))  42.1 us
    all_gather x4, blocking collectives, apply_operator(): pair_loads = lax.all_gather(weighted, 'tgt', axis=1, tiled=True)  18.3 us
    reduce_sum x8, other arithmetic, stokes_block(): square = jnp.sum(offset * offset, axis=0) + soften  14.6 us

commit v1 on v0

v1 whole, which is shorter than its diff:
```python
import functools

import jax
import jax.numpy as jnp
from jax import lax
from jax.experimental import pallas as pl
from jax.experimental.pallas import tpu as pltpu
from jax.sharding import PartitionSpec as P

ITERS = 4
soften = 0.0025
MESH = pl.DeviceIdType.MESH
CACHE_BYTES = 24 * 2**20


def total(value):
    while value.ndim > 2:
        value = jnp.sum(value, axis=0)
    return jnp.sum(jnp.sum(value, axis=0, keepdims=True), axis=1, keepdims=True)


def pair_tables(targets, sources):
    r = [t - s for t, s in zip(targets, sources)]
    square = r[0] * r[0] + r[1] * r[1] + r[2] * r[2] + soften
    inverse = lax.rsqrt(square)
    factor = inverse * inverse * inverse
    root = inverse * inverse * lax.rsqrt(inverse)
    near = factor * (square + soften)
    return near, [root * c for c in r]


def flip(index, mask, bits):
    out = index
    for b in range(bits):
        if isinstance(mask, int):
            chosen = (mask >> b) & 1
            if not chosen:
                continue
        else:
            chosen = lax.rem(lax.div(mask, 1 << b), 2)
        mine = lax.rem(lax.div(index, 1 << b), 2)
        out = out + chosen * (1 - 2 * mine) * (1 << b)
    return out


def kernel(
    S, T, L, cached, group,
    pos_ref, area_ref, rhs_ref, sol_ref, res_ref, hess_ref,
    geo, wbuf, basis, acc, tcol, tables, send_sem, recv_sem,
):
    D = S * T
    bits = D.bit_length() - 1
    me = lax.axis_index("src") * T + lax.axis_index("tgt")
    group_bits = group.bit_length() - 1
    low_me = [flip(lax.rem(me, group), j, group_bits) for j in range(group)]
    high_me = lax.div(me, group)

    def coords(p):
        return (lax.div(p, T), lax.rem(p, T))

    barrier = pltpu.get_barrier_semaphore()

    def greet(s, unused):
        high = flip(high_me, s, bits - group_bits)
        for j in range(group):
            p = high * group + low_me[j]

            def signal():
                pl.semaphore_signal(barrier, inc=1, device_id=coords(p), device_id_type=MESH)

            if j == 0:
                pl.when(s > 0)(signal)
            else:
                signal()
        return unused

    lax.fori_loop(0, D // group, greet, 0)

    coefficient = float(L * D) ** (-0.5)
    geo[me, 0:3, :] = pos_ref[...]
    geo[me, 3:4, :] = area_ref[...] * coefficient
    geo[me, 4:7, :] = rhs_ref[...]
    geo[me, 7:8, :] = jnp.zeros((1, L), jnp.float32)
    for a in range(3):
        tcol[a] = jnp.broadcast_to(pos_ref[a : a + 1, :], (L, L)).T
    pl.semaphore_wait(barrier, D - 1)

    def copy(buffer, phase, source, dest):
        return pltpu.make_async_remote_copy(
            src_ref=buffer.at[source],
            dst_ref=buffer.at[source],
            send_sem=send_sem.at[phase],
            recv_sem=recv_sem.at[phase, source],
            device_id=coords(dest),
            device_id_type=MESH,
        )

    def send_all(buffer, phase):
        def step(i, unused):
            high = flip(high_me, D // group - 1 - i, bits - group_bits)
            for j in reversed(range(group)):
                copy(buffer, phase, me, high * group + low_me[j]).start()
            return unused

        lax.fori_loop(0, D // group - 1, step, 0)
        for j in reversed(range(1, group)):
            copy(buffer, phase, me, high_me * group + low_me[j]).start()

    rows = 32 if L % 32 == 0 else L

    def blocks_of(high):
        return [high * group + low_me[j] for j in range(group)]

    def absorb(high, density, first, fresh):
        ps = blocks_of(high)
        qs = [density(p) * geo[p, 3:4, :] for p in ps]
        for r0 in range(0, L, rows):
            span = pl.ds(r0, rows)
            sums = None if fresh else [acc[a, span, :] for a in range(3)]
            for p, q in zip(ps, qs):
                q = [q[a : a + 1, :] for a in range(3)]
                if cached and not first:
                    near = tables[0, p, span, :]
                    g = [tables[1 + a, p, span, :] for a in range(3)]
                else:
                    near, g = pair_tables(
                        [tcol[a, span, :] for a in range(3)], [geo[p, a : a + 1, :] for a in range(3)]
                    )
                    if cached:
                        tables[0, p, span, :] = near
                        for a in range(3):
                            tables[1 + a, p, span, :] = g[a]
                along = g[0] * q[0] + g[1] * q[1] + g[2] * q[2]
                terms = [near * q[a] + g[a] * along for a in range(3)]
                sums = terms if sums is None else [x + y for x, y in zip(sums, terms)]
            for a in range(3):
                acc[a, span, :] = sums[a]

    def receive(buffer, phase, density, first, compute):
        for j in range(1, group):
            p = high_me * group + low_me[j]
            copy(buffer, phase, p, p).wait_recv()
        if compute:
            absorb(high_me, density, first, True)

        def step(s, unused):
            high = flip(high_me, s, bits - group_bits)
            for j in range(group):
                p = high * group + low_me[j]
                copy(buffer, phase, p, p).wait_recv()
            if compute:
                absorb(high, density, first, False)
            return unused

        lax.fori_loop(1, D // group, step, 0)
        if compute:
            return jnp.concatenate(
                [jnp.sum(acc[a].T, axis=0, keepdims=True) for a in range(3)], axis=0
            )
        return None

    send_all(geo, 0)
    induced = receive(geo, 0, lambda p: geo[p, 4:7, :], True, True)
    own = rhs_ref[...] + induced
    wbuf[0, me] = own
    send_all(wbuf.at[0], 1)

    full = geo[:, 4:7, :]
    initial = jnp.sqrt(total(full * full))
    scale = 1.0 / initial
    basis[0] = full * scale
    mine = [rhs_ref[...] * scale]

    zero = jnp.zeros((1, 1), jnp.float32)
    hess = [[zero] * ITERS for _ in range(ITERS + 1)]
    triangle = [[zero] * ITERS for _ in range(ITERS)]
    target = [initial] + [zero] * ITERS
    rotations = []
    applied_mine = []
    for k in range(ITERS):
        last = k == ITERS - 1
        induced = receive(wbuf.at[k], k + 1, lambda p: wbuf[k, p], False, not last)
        applied = wbuf[k] * scale
        applied_mine.append(own * scale)
        projections = [total(basis[i] * applied) for i in range(k + 1)]
        if not last:
            own = (own + induced) * scale
            for i in range(k + 1):
                own = own - projections[i] * applied_mine[i]
            wbuf[k + 1, me] = own
            send_all(wbuf.at[k + 1], k + 2)
        remainder = applied
        removed = projections[0] * basis[0]
        removed_mine = projections[0] * mine[0]
        for i in range(1, k + 1):
            removed = removed + projections[i] * basis[i]
            removed_mine = removed_mine + projections[i] * mine[i]
        remainder = applied - removed
        height = jnp.sqrt(total(remainder * remainder))
        scale = 1.0 / height
        if not last:
            basis[k + 1] = remainder * scale
        mine.append((applied_mine[k] - removed_mine) * scale)
        for i in range(k + 1):
            hess[i][k] = projections[i]
        hess[k + 1][k] = height
        column = list(projections)
        for i, (cosine, sine) in enumerate(rotations):
            top, low = column[i], column[i + 1]
            column[i] = cosine * top + sine * low
            column[i + 1] = cosine * low - sine * top
        leading = column[k]
        radius = jnp.sqrt(leading * leading + height * height)
        cosine, sine = leading / radius, height / radius
        rotations.append((cosine, sine))
        column[k] = cosine * leading + sine * height
        for i in range(k + 1):
            triangle[i][k] = column[i]
        top = target[k]
        target[k] = cosine * top
        target[k + 1] = -sine * top

    y = [None] * ITERS
    for i in reversed(range(ITERS)):
        left = target[i]
        for j in range(i + 1, ITERS):
            left = left - triangle[i][j] * y[j]
        y[i] = left / triangle[i][i]
    solution_field = y[0] * mine[0]
    for i in range(1, ITERS):
        solution_field = solution_field + y[i] * mine[i]
    sol_ref[...] = solution_field
    residual = None
    for i in range(ITERS + 1):
        gap = initial if i == 0 else zero
        for j in range(max(i - 1, 0), ITERS):
            gap = gap - hess[i][j] * y[j]
        term = gap * mine[i]
        residual = term if residual is None else residual + term
    res_ref[...] = residual
    row = lax.broadcasted_iota(jnp.int32, (ITERS + 1, ITERS), 0)
    col = lax.broadcasted_iota(jnp.int32, (ITERS + 1, ITERS), 1)
    table = jnp.zeros((ITERS + 1, ITERS), jnp.float32)
    for k in range(ITERS):
        for i in range(k + 2):
            table = jnp.where((row == i) & (col == k), hess[i][k], table)
    hess_ref[...] = table

    for phase in range(ITERS + 1):
        buffer = geo if phase == 0 else wbuf.at[phase - 1]
        everyone = buffer.at[pl.ds(0, D - 1)]
        pltpu.make_async_remote_copy(
            src_ref=everyone,
            dst_ref=everyone,
            send_sem=send_sem.at[phase],
            recv_sem=recv_sem.at[phase, me],
            device_id=coords(me),
            device_id_type=MESH,
        ).wait_send()


def local(S, T, positions, areas, right_side):
    L = positions.shape[1]
    D = S * T
    group = 4
    cached = 4 * D * L * L * 4 <= CACHE_BYTES
    f32 = jnp.float32
    return pl.pallas_call(
        functools.partial(kernel, S, T, L, cached, group),
        out_shape=(
            jax.ShapeDtypeStruct((3, L), f32),
            jax.ShapeDtypeStruct((3, L), f32),
            jax.ShapeDtypeStruct((ITERS + 1, ITERS), f32),
        ),
        in_specs=[pl.BlockSpec(memory_space=pltpu.VMEM)] * 3,
        out_specs=(pl.BlockSpec(memory_space=pltpu.VMEM),) * 3,
        scratch_shapes=[
            pltpu.VMEM((D, 8, L), f32),
            pltpu.VMEM((ITERS, D, 3, L), f32),
            pltpu.VMEM((ITERS, D, 3, L), f32),
            pltpu.VMEM((3, L, L), f32),
            pltpu.VMEM((3, L, L), f32),
            pltpu.VMEM((4, D, L, L) if cached else (1, 1, 8, 128), f32),
            pltpu.SemaphoreType.DMA((ITERS + 1,)),
            pltpu.SemaphoreType.DMA((ITERS + 1, D)),
        ],
        compiler_params=pltpu.CompilerParams(
            collective_id=0, has_side_effects=True, vmem_limit_bytes=48 * 2**20
        ),
    )(positions, areas.reshape(1, L), right_side)


def solution(mesh):
    S, T = mesh.shape["src"], mesh.shape["tgt"]
    return jax.shard_map(
        functools.partial(local, S, T),
        mesh=mesh,
        in_specs=(P(None, ("src", "tgt")), P(("src", "tgt")), P(None, ("src", "tgt"))),
        out_specs=(P(None, ("src", "tgt")), P(None, ("src", "tgt")), P()),
        check_vma=False,
    )
```

time: 613 us -> 39.1 us (0.06)
  blocking collectives: 523 us -> 0 us
  other arithmetic: 43.4 us -> 0 us
  Pallas kernels: 0 us -> 34.5 us
  between operations: 27.7 us -> 0.65 us
  local copies, waits for them, and re-layouts: 15.9 us -> 3.83 us
    psum x9 -> x0, blocking collectives: 358 us -> none  [the longest x4 168 us: local(): height = jnp.sqrt(lax.psum(jnp.sum(remainder * remainder), ('src', 'tgt')))]
    all_gather x9 -> x0, blocking collectives: 165 us -> none  [the longest x4 82.6 us: apply_operator(): lax.all_gather(a, 'src', axis=1, tiled=True)]
    pallas_call x0 -> x1, Pallas kernels: none -> 34.5 us  [local(): pl.pallas_call(functools.partial(kernel, S, T, L, cached, group), out_sha...]
    reduce_sum x32 -> x0, other arithmetic: 28.9 us -> none  [the longest x8 14.6 us: stokes_block(): square = jnp.sum(offset * offset, axis=0) + soften]
    another operation x12 -> x0, other arithmetic: 8.71 us -> none
    slice x12 -> x0, local copies, waits for them, and re-layouts: 6.13 us -> none  [the longest x4 2.31 us: least_squares(): leading = triangle[column, column]]
where the time goes in v1:
time: 39.1 us; the launch traced here: 39 us
  Pallas kernels  34.5 us (88%)
  local copies, waits for them, and re-layouts  3.83 us (10%)
  between operations  0.65 us (2%)
    pallas_call x1, Pallas kernels, local(): pl.pallas_call(functools.partial(kernel, S, T, L, cached, group), out_sha...  34.5 us
    unnamed x8, local copies, waits for them, and re-layouts  3.17 us

profile of v1, /device:TPU:0, one launch (start us, length us, event | category | flops | bytes accessed | tf_op | source)
XLA Modules:
  0.0 39.0 jit_solution(14912531452148574911)
XLA Ops:
  0.6 0.0 copy-start.2
  0.6 0.6 %copy-done.2 = f32[128]{0:T(128)S(1)} copy-done((f32[128]{0:T(128)S(1)}, f32[128]{0:T(128)}, u32[]{:S(2)}) %copy-start.2) | copy-done | bytes 536
  1.3 0.0 copy-start
  1.3 0.7 %copy-done = f32[3,128]{1,0:T(4,128)S(1)} copy-done((f32[3,128]{1,0:T(4,128)S(1)}, f32[3,128]{1,0:T(4,128)}, u32[]{:S(2)}) %copy-start) | copy-done | bytes 1560
  2.0 0.0 copy-start.1
  2.0 0.7 %copy-done.1 = f32[3,128]{1,0:T(4,128)S(1)} copy-done((f32[3,128]{1,0:T(4,128)S(1)}, f32[3,128]{1,0:T(4,128)}, u32[]{:S(2)}) %copy-start.1) | copy-done | bytes 1560
  2.7 34.5 %shard_map.58 = (f32[3,128]{1,0:T(4,128)S(1)}, f32[3,128]{1,0:T(4,128)S(1)}, f32[5,4]{1,0:T(8,128)S(1)}) custom-call(f32[3,128]{1,0:T(4,128)S(1)} %copy-done, f32[1,128]{1,0:T(1,128)S(1)} %bitcast.1, f32[3,128]{1,0:T(4,128)S(1)} %copy-done.1), custom_call_target="tpu_custom_call" | custom-call | tf_op jit(solution)/shard_map/pallas_call | solution.py:268
  37.1 0.7 %copy.6 = f32[5,4]{0,1:T(4,128)} copy(f32[5,4]{1,0:T(8,128)S(1)} %get-tuple-element.5) | data formatting | bytes 160 | tf_op jit(solution)/shard_map/pallas_call | solution.py:268
  37.8 0.6 %copy.9 = f32[3,128]{1,0:T(4,128)} copy(f32[3,128]{1,0:T(4,128)S(1)} %get-tuple-element.9) | data formatting | bytes 3072
  38.4 0.6 %copy.10 = f32[3,128]{1,0:T(4,128)} copy(f32[3,128]{1,0:T(4,128)S(1)} %get-tuple-element.10) | data formatting | bytes 3072
Async XLA Ops:
  0.6 0.7 %copy-start.2 = (f32[128]{0:T(128)S(1)}, f32[128]{0:T(128)}, u32[]{:S(2)}) copy-start(f32[128]{0:T(128)} %param.4) | copy-start | bytes 1540
  1.3 0.7 %copy-start = (f32[3,128]{1,0:T(4,128)S(1)}, f32[3,128]{1,0:T(4,128)}, u32[]{:S(2)}) copy-start(f32[3,128]{1,0:T(4,128)} %pos_ref.1) | copy-start | bytes 4612
  2.0 0.7 %copy-start.1 = (f32[3,128]{1,0:T(4,128)S(1)}, f32[3,128]{1,0:T(4,128)}, u32[]{:S(2)}) copy-start(f32[3,128]{1,0:T(4,128)} %rhs_ref.1) | copy-start | bytes 4612

commit v2 on v1

--- a/solution.py
+++ b/solution.py
@@ -45,8 +45,9 @@
 
 def kernel(
     S, T, L, cached, group,
-    pos_ref, area_ref, rhs_ref, sol_ref, res_ref, hess_ref,
-    geo, wbuf, basis, acc, tcol, tables, send_sem, recv_sem,
+    pos_in, area_in, rhs_in, out_ref,
+    pos_ref, area_ref, rhs_ref, geo, wbuf, whole, basis, acc, tcol, tables,
+    load_sem, send_sem, recv_sem,
 ):
     D = S * T
     bits = D.bit_length() - 1
@@ -75,6 +76,14 @@
         return unused
 
     lax.fori_loop(0, D // group, greet, 0)
+    loads = [
+        pltpu.make_async_copy(x, y, load_sem.at[i])
+        for i, (x, y) in enumerate([(pos_in, pos_ref), (area_in, area_ref), (rhs_in, rhs_ref)])
+    ]
+    for load in loads:
+        load.start()
+    for load in loads:
+        load.wait()
 
     coefficient = float(L * D) ** (-0.5)
     geo[me, 0:3, :] = pos_ref[...]
@@ -177,19 +186,28 @@
     target = [initial] + [zero] * ITERS
     rotations = []
     applied_mine = []
+    sent = [own]
     for k in range(ITERS):
         last = k == ITERS - 1
         induced = receive(wbuf.at[k], k + 1, lambda p: wbuf[k, p], False, not last)
-        applied = wbuf[k] * scale
-        applied_mine.append(own * scale)
-        projections = [total(basis[i] * applied) for i in range(k + 1)]
         if not last:
-            own = (own + induced) * scale
-            for i in range(k + 1):
-                own = own - projections[i] * applied_mine[i]
+            own = own + induced
+            for i in range(k):
+                own = own - hess[i][k - 1] * sent[i + 1]
+            own = own * scale
             wbuf[k + 1, me] = own
             send_all(wbuf.at[k + 1], k + 2)
-        remainder = applied
+            sent.append(own)
+        applied = wbuf[k]
+        mine_now = wbuf[k, me]
+        for i in range(k):
+            applied = applied - hess[i][k - 1] * whole[i]
+            mine_now = mine_now - hess[i][k - 1] * applied_mine[i]
+        applied = applied * scale
+        applied_mine.append(mine_now * scale)
+        if not last:
+            whole[k] = applied
+        projections = [total(basis[i] * applied) for i in range(k + 1)]
         removed = projections[0] * basis[0]
         removed_mine = projections[0] * mine[0]
         for i in range(1, k + 1):
@@ -229,7 +247,7 @@
     solution_field = y[0] * mine[0]
     for i in range(1, ITERS):
         solution_field = solution_field + y[i] * mine[i]
-    sol_ref[...] = solution_field
+    out_ref[0:3, :] = solution_field
     residual = None
     for i in range(ITERS + 1):
         gap = initial if i == 0 else zero
@@ -237,14 +255,14 @@
             gap = gap - hess[i][j] * y[j]
         term = gap * mine[i]
         residual = term if residual is None else residual + term
-    res_ref[...] = residual
-    row = lax.broadcasted_iota(jnp.int32, (ITERS + 1, ITERS), 0)
-    col = lax.broadcasted_iota(jnp.int32, (ITERS + 1, ITERS), 1)
-    table = jnp.zeros((ITERS + 1, ITERS), jnp.float32)
+    out_ref[8:11, :] = residual
+    row = lax.broadcasted_iota(jnp.int32, (8, L), 0)
+    col = lax.broadcasted_iota(jnp.int32, (8, L), 1)
+    table = jnp.zeros((8, L), jnp.float32)
     for k in range(ITERS):
         for i in range(k + 2):
-            table = jnp.where((row == i) & (col == k), hess[i][k], table)
-    hess_ref[...] = table
+            table = jnp.where((row == k) & (col == i), hess[i][k], table)
+    out_ref[16:24, :] = table
 
     for phase in range(ITERS + 1):
         buffer = geo if phase == 0 else wbuf.at[phase - 1]
@@ -259,35 +277,55 @@
         ).wait_send()
 
 
+def unpack(packed_ref, sol_ref, res_ref, hess_ref):
+    sol_ref[...] = packed_ref[0:3, :]
+    res_ref[...] = packed_ref[8:11, :]
+    hess_ref[...] = packed_ref[16 : 16 + ITERS, 0 : ITERS + 1]
+
+
 def local(S, T, positions, areas, right_side):
     L = positions.shape[1]
     D = S * T
     group = 4
     cached = 4 * D * L * L * 4 <= CACHE_BYTES
     f32 = jnp.float32
-    return pl.pallas_call(
+    vmem = pl.BlockSpec(memory_space=pltpu.VMEM)
+    packed = pl.pallas_call(
         functools.partial(kernel, S, T, L, cached, group),
-        out_shape=(
-            jax.ShapeDtypeStruct((3, L), f32),
-            jax.ShapeDtypeStruct((3, L), f32),
-            jax.ShapeDtypeStruct((ITERS + 1, ITERS), f32),
-        ),
-        in_specs=[pl.BlockSpec(memory_space=pltpu.VMEM)] * 3,
-        out_specs=(pl.BlockSpec(memory_space=pltpu.VMEM),) * 3,
+        out_shape=jax.ShapeDtypeStruct((24, L), f32),
+        in_specs=[pl.BlockSpec(memory_space=pltpu.HBM)] * 3,
+        out_specs=vmem,
         scratch_shapes=[
+            pltpu.VMEM((3, L), f32),
+            pltpu.VMEM((1, L), f32),
+            pltpu.VMEM((3, L), f32),
             pltpu.VMEM((D, 8, L), f32),
             pltpu.VMEM((ITERS, D, 3, L), f32),
+            pltpu.VMEM((ITERS - 1, D, 3, L), f32),
             pltpu.VMEM((ITERS, D, 3, L), f32),
             pltpu.VMEM((3, L, L), f32),
             pltpu.VMEM((3, L, L), f32),
             pltpu.VMEM((4, D, L, L) if cached else (1, 1, 8, 128), f32),
+            pltpu.SemaphoreType.DMA((3,)),
             pltpu.SemaphoreType.DMA((ITERS + 1,)),
             pltpu.SemaphoreType.DMA((ITERS + 1, D)),
         ],
         compiler_params=pltpu.CompilerParams(
-            collective_id=0, has_side_effects=True, vmem_limit_bytes=48 * 2**20
+            collective_id=0, has_side_effects=True, vmem_limit_bytes=67043328
         ),
     )(positions, areas.reshape(1, L), right_side)
+    field, residual, columns = pl.pallas_call(
+        unpack,
+        out_shape=(
+            jax.ShapeDtypeStruct((3, L), f32),
+            jax.ShapeDtypeStruct((3, L), f32),
+            jax.ShapeDtypeStruct((ITERS, ITERS + 1), f32),
+        ),
+        in_specs=[vmem],
+        out_specs=(vmem,) * 3,
+        compiler_params=pltpu.CompilerParams(vmem_limit_bytes=2**20),
+    )(packed)
+    return field, residual, columns.T
 
 
 def solution(mesh):

time: 39.1 us -> 38 us (0.972)
  local copies, waits for them, and re-layouts: 3.83 us -> 0.7 us
  Pallas kernels: 34.5 us -> 36.4 us
    unnamed x8 -> x2, local copies, waits for them, and re-layouts: 3.17 us -> 0.7 us
    pallas_call x1, Pallas kernels: 34.5 us -> 35.8 us  [local(): pl.pallas_call(functools.partial(kernel, S, T, L, cached, group), out_sha...]
    pallas_call x1 -> x0, local copies, waits for them, and re-layouts: 0.66 us -> none  [local(): pl.pallas_call(functools.partial(kernel, S, T, L, cached, group), out_sha...]
    pallas_call x0 -> x1, Pallas kernels: none -> 0.59 us  [local(): pl.pallas_call(unpack, out_shape=(jax.ShapeDtypeStruct((3, L), f32), jax....]
where the time goes in v2:
time: 38 us; the launch traced here: 37.7 us
  Pallas kernels  36.4 us (96%)
  local copies, waits for them, and re-layouts  0.7 us (2%)
  between operations  0.65 us (2%)
    pallas_call x1, Pallas kernels, local(): pl.pallas_call(functools.partial(kernel, S, T, L, cached, group), out_sha...  35.8 us

profile of v2, /device:TPU:0, one launch (start us, length us, event | category | flops | bytes accessed | tf_op | source)
XLA Modules:
  0.0 37.7 jit_solution(8661770384194124199)
XLA Ops:
  0.6 35.8 %shard_map.58.packed_ref = f32[24,128]{1,0:T(8,128)} custom-call(f32[3,128]{1,0:T(4,128)} %pos_in.1, f32[1,128]{1,0:T(1,128)} %bitcast.2, f32[3,128]{1,0:T(4,128)} %rhs_in.1), custom_call_target="tpu_custom_call" | custom-call | tf_op jit(solution)/shard_map/pallas_call | solution.py:293
  36.4 0.0 copy-start
  36.4 0.7 %copy-done = f32[24,128]{1,0:T(8,128)S(1)} copy-done((f32[24,128]{1,0:T(8,128)S(1)}, f32[24,128]{1,0:T(8,128)}, u32[]{:S(2)}) %copy-start) | copy-done | bytes 12312
  37.1 0.6 %shard_map.59 = (f32[3,128]{1,0:T(4,128)}, f32[3,128]{1,0:T(4,128)}, f32[4,5]{1,0:T(4,128)}) custom-call(f32[24,128]{1,0:T(8,128)S(1)} %copy-done), custom_call_target="tpu_custom_call" | custom-call | tf_op jit(solution)/shard_map/pallas_call | solution.py:317
Async XLA Ops:
  36.4 0.7 %copy-start = (f32[24,128]{1,0:T(8,128)S(1)}, f32[24,128]{1,0:T(8,128)}, u32[]{:S(2)}) copy-start(f32[24,128]{1,0:T(8,128)} %shard_map.58.packed_ref) | copy-start | bytes 36868

commit v3 on v2

--- a/solution.py
+++ b/solution.py
@@ -27,6 +27,14 @@
     root = inverse * inverse * lax.rsqrt(inverse)
     near = factor * (square + soften)
     return near, [root * c for c in r]
+
+
+def pair_terms(targets, sources):
+    r = [t - s for t, s in zip(targets, sources)]
+    square = r[0] * r[0] + r[1] * r[1] + r[2] * r[2] + soften
+    inverse = lax.rsqrt(square)
+    factor = inverse * inverse * inverse
+    return factor * (square + soften), factor, r
 
 
 def flip(index, mask, bits):
@@ -132,14 +140,12 @@
                     near = tables[0, p, span, :]
                     g = [tables[1 + a, p, span, :] for a in range(3)]
                 else:
-                    near, g = pair_tables(
+                    near, factor, g = pair_terms(
                         [tcol[a, span, :] for a in range(3)], [geo[p, a : a + 1, :] for a in range(3)]
                     )
-                    if cached:
-                        tables[0, p, span, :] = near
-                        for a in range(3):
-                            tables[1 + a, p, span, :] = g[a]
                 along = g[0] * q[0] + g[1] * q[1] + g[2] * q[2]
+                if first or not cached:
+                    along = along * factor
                 terms = [near * q[a] + g[a] * along for a in range(3)]
                 sums = terms if sums is None else [x + y for x, y in zip(sums, terms)]
             for a in range(3):
@@ -173,6 +179,21 @@
     own = rhs_ref[...] + induced
     wbuf[0, me] = own
     send_all(wbuf.at[0], 1)
+
+    def build(high, unused):
+        for p in blocks_of(high):
+            for r0 in range(0, L, rows):
+                span = pl.ds(r0, rows)
+                near, g = pair_tables(
+                    [tcol[a, span, :] for a in range(3)], [geo[p, a : a + 1, :] for a in range(3)]
+                )
+                tables[0, p, span, :] = near
+                for a in range(3):
+                    tables[1 + a, p, span, :] = g[a]
+        return unused
+
+    if cached:
+        lax.fori_loop(0, D // group, build, 0)
 
     full = geo[:, 4:7, :]
     initial = jnp.sqrt(total(full * full))

time: 38 us -> 37.4 us (0.984)
  Pallas kernels: 36.4 us -> 35.8 us
    pallas_call x1, Pallas kernels: 35.8 us -> 35.2 us  [local(): pl.pallas_call(functools.partial(kernel, S, T, L, cached, group), out_sha...]
where the time goes in v3:
time: 37.4 us; the launch traced here: 37.1 us
  Pallas kernels  35.8 us (96%)
  local copies, waits for them, and re-layouts  0.7 us (2%)
  between operations  0.65 us (2%)
    pallas_call x1, Pallas kernels, local(): pl.pallas_call(functools.partial(kernel, S, T, L, cached, group), out_sha...  35.2 us

profile of v3, /device:TPU:0, one launch (start us, length us, event | category | flops | bytes accessed | tf_op | source)
XLA Modules:
  0.0 37.1 jit_solution(16466795786398002705)
XLA Ops:
  0.6 35.2 %shard_map.58.packed_ref = f32[24,128]{1,0:T(8,128)} custom-call(f32[3,128]{1,0:T(4,128)} %pos_in.1, f32[1,128]{1,0:T(1,128)} %bitcast.2, f32[3,128]{1,0:T(4,128)} %rhs_in.1), custom_call_target="tpu_custom_call" | custom-call | tf_op jit(solution)/shard_map/pallas_call | solution.py:314
  35.8 0.0 copy-start
  35.8 0.7 %copy-done = f32[24,128]{1,0:T(8,128)S(1)} copy-done((f32[24,128]{1,0:T(8,128)S(1)}, f32[24,128]{1,0:T(8,128)}, u32[]{:S(2)}) %copy-start) | copy-done | bytes 12312
  36.5 0.6 %shard_map.59 = (f32[3,128]{1,0:T(4,128)}, f32[3,128]{1,0:T(4,128)}, f32[4,5]{1,0:T(4,128)}) custom-call(f32[24,128]{1,0:T(8,128)S(1)} %copy-done), custom_call_target="tpu_custom_call" | custom-call | tf_op jit(solution)/shard_map/pallas_call | solution.py:338
Async XLA Ops:
  35.8 0.7 %copy-start = (f32[24,128]{1,0:T(8,128)S(1)}, f32[24,128]{1,0:T(8,128)}, u32[]{:S(2)}) copy-start(f32[24,128]{1,0:T(8,128)} %shard_map.58.packed_ref) | copy-start | bytes 36868
